TPU v7x, 32 devices: a whole 2x2x4 slice. The times are simulated.
32 devices in a mesh: seq: 8 (over y, x, core), kvh: 4 (over z).
Axes of the slice: x: 2, y: 2, z: 4, core: 2. Of those that a mesh axis runs over, the one named last changes fastest.
Arguments:
- queries: bfloat16 [64, 32, 128], P(('seq', 'kvh')), may hold values from -9 to 9
- attn_out: bfloat16 [64, 32, 128], P(('seq', 'kvh')), may hold values from -0.59765625 to 0.59765625
- grad_out: bfloat16 [64, 32, 128], P(('seq', 'kvh')), may hold values from -384 to 384
- log_norms: float32 [64, 32], P(('seq', 'kvh')), may hold values from 0 to 14, as said below
- query_starts: int32 [64], replicated, may hold values from 0 to 2048
- keys: bfloat16 [8192, 4, 128], P('seq', 'kvh'), may hold values from -6 to 6
- values: bfloat16 [8192, 4, 128], P('seq', 'kvh'), may hold values from -6 to 6
Outputs:
- grad_query: bfloat16 [64, 32, 128], P(('seq', 'kvh'))
- grad_keys: bfloat16 [8192, 4, 128], P('seq', 'kvh')
- grad_values: bfloat16 [8192, 4, 128], P('seq', 'kvh')
Inputs may be any that keep to these rules, and one draw needn't show every extreme that they name: `log_norms`: each entry lies within one of the log of its token's number of visible positions plus 1.125.
All inputs are finite; a program needn't handle non-finite values.
Results may differ from a plain program's by a relative error of at most 0.0052.
Values may be sent and summed in bfloat16 or wider, within the bound.
No kernel may reach another device: no remote copies, remote signals or barrier semaphores. Data moves between devices by JAX's collectives and lax.ppermute only.
A program may use at most 64 MiB of HBM per device.

v0:
```python
import jax
import jax.numpy as jnp
from jax import lax
from jax.sharding import PartitionSpec as P


def shifted(value, axis, by):
    peers = lax.axis_size(axis)
    return lax.ppermute(value, axis, [(i, (i + by) % peers) for i in range(peers)])


def local(queries, attn_out, grad_out, log_norms, query_starts, keys, values):
    scaling = queries.shape[-1] ** (-0.5)
    seq_count = lax.axis_size("seq")
    seq_index = lax.axis_index("seq")
    deltas = jnp.sum(grad_out.astype(jnp.float32) * attn_out.astype(jnp.float32), axis=-1)
    query_block, grad_block = (
        lax.all_to_all(queries, "kvh", split_axis=1, concat_axis=0, tiled=True),
        lax.all_to_all(grad_out, "kvh", split_axis=1, concat_axis=0, tiled=True),
    )
    norm_block, delta_block = (
        lax.all_to_all(log_norms, "kvh", split_axis=1, concat_axis=0, tiled=True),
        lax.all_to_all(deltas, "kvh", split_axis=1, concat_axis=0, tiled=True),
    )
    block_rows = query_block.shape[0]
    total_rows = block_rows * seq_count
    key_count = keys.shape[0]
    key_rows = keys[:, 0, :]
    value_rows = values[:, 0, :]
    key_pos = seq_index * key_count + jnp.arange(key_count, dtype=jnp.int32)
    offset = key_count * seq_count - total_rows

    def block_terms(queries_in, grads_in, norms_in, deltas_in, first_row):
        row_count = queries_in.shape[0]
        query_pos = offset + first_row + jnp.arange(row_count, dtype=jnp.int32)
        first_keys = lax.dynamic_slice_in_dim(query_starts, first_row, row_count)
        visible = (key_pos[None, :] >= first_keys[:, None]) & (
            key_pos[None, :] <= query_pos[:, None]
        )
        scores = (
            jnp.einsum("rgd,kd->rgk", queries_in, key_rows, preferred_element_type=jnp.float32)
            * scaling
        )
        weights = jnp.where(visible[:, None, :], jnp.exp(scores - norms_in[..., None]), 0.0)
        weight_grad = jnp.einsum(
            "rgd,kd->rgk", grads_in, value_rows, preferred_element_type=jnp.float32
        )
        score_grad = weights * (weight_grad - deltas_in[..., None])
        weight_half = weights.astype(jnp.bfloat16)
        score_half = score_grad.astype(jnp.bfloat16)
        value_part = jnp.einsum(
            "rgk,rgd->kd", weight_half, grads_in, preferred_element_type=jnp.float32
        )
        key_part = (
            jnp.einsum("rgk,rgd->kd", score_half, queries_in, preferred_element_type=jnp.float32)
            * scaling
        )
        query_part = (
            jnp.einsum("rgk,kd->rgd", score_half, key_rows, preferred_element_type=jnp.float32)
            * scaling
        )
        return (key_part, value_part, query_part)

    key_empty = jnp.zeros(key_rows.shape, jnp.float32)

    def visit_owner(counter, carried):
        query_now, grad_now, norm_now, delta_now, query_grad, key_grad, value_grad = carried
        anchor = (seq_index - counter) % seq_count
        key_part, value_part, query_part = block_terms(
            query_now, grad_now, norm_now, delta_now, anchor * block_rows
        )
        query_now, grad_now = shifted((query_now, grad_now), "seq", 1)
        norm_now, delta_now, query_grad = shifted(
            (norm_now, delta_now, query_grad + query_part), "seq", 1
        )
        return (
            query_now,
            grad_now,
            norm_now,
            delta_now,
            query_grad,
            key_grad + key_part,
            value_grad + value_part,
        )

    query_empty = jnp.zeros(query_block.shape, jnp.float32)
    carried = (query_block, grad_block, norm_block, delta_block, query_empty, key_empty, key_empty)
    carried = lax.fori_loop(0, seq_count - 1, visit_owner, carried)
    query_now, grad_now, norm_now, delta_now, query_grad, key_grad, value_grad = carried
    anchor = (seq_index + 1) % seq_count
    key_part, value_part, query_part = block_terms(
        query_now, grad_now, norm_now, delta_now, anchor * block_rows
    )
    key_grad = key_grad + key_part
    value_grad = value_grad + value_part
    query_grad = shifted((query_grad + query_part).astype(jnp.bfloat16), "seq", 1).astype(
        jnp.float32
    )
    grad_query = lax.all_to_all(
        query_grad.astype(jnp.bfloat16), "kvh", split_axis=0, concat_axis=1, tiled=True
    )
    return (
        grad_query,
        key_grad.astype(jnp.bfloat16)[:, None, :],
        value_grad.astype(jnp.bfloat16)[:, None, :],
    )


def solution(mesh):
    return jax.shard_map(
        local,
        mesh=mesh,
        in_specs=(
            P(("seq", "kvh"), None, None),
            P(("seq", "kvh"), None, None),
            P(("seq", "kvh"), None, None),
            P(("seq", "kvh"), None),
            P(),
            P("seq", "kvh", None),
            P("seq", "kvh", None),
        ),
        out_specs=(P(("seq", "kvh"), None, None), P("seq", "kvh", None), P("seq", "kvh", None)),
        check_vma=False,
    )
```

profile of v0, /device:TPU:0, one launch (start us, length us, event | category | flops | bytes accessed | tf_op | source)
XLA Modules:
  0.0 116.3 jit_solution(9681202412714350968)
XLA Ops:
  2.1 6.3 %all-to-all-start.2 = ((f32[2,4,8]{2,0,1:T(2,128)}), f32[2,4,8]{2,0,1:T(2,128)S(1)}, u32[]{:S(2)}, u32[]{:S(2)}) async-start(f32[2,4,8]{2,0,1:T(2,128)} %copy.31), calls=%async_computation.2 | async-start | bytes 8192 | tf_op jit(solution)/shard_map/all_to_all | solution.py:22
  9.8 4.2 %all-to-all-done.2 = f32[2,4,8]{2,0,1:T(2,128)S(1)} async-done(((f32[2,4,8]{2,0,1:T(2,128)}), f32[2,4,8]{2,0,1:T(2,128)S(1)}, u32[]{:S(2)}, u32[]{:S(2)}) %all-to-all-start.2) | async-done | bytes 288 | tf_op jit(solution)/shard_map/all_to_all | solution.py:22
  14.0 3.3 %all-to-all-start = ((bf16[2,32,128]{2,0,1:T(2,128)(2,1)}), bf16[2,32,128]{2,0,1:T(2,128)(2,1)S(1)}, u32[]{:S(2)}, u32[]{:S(2)}) async-start(bf16[2,32,128]{2,0,1:T(2,128)(2,1)} %copy.27), calls=%async_computation | async-start | bytes 32768 | tf_op jit(solution)/shard_map/all_to_all | solution.py:18
  18.7 4.2 %all-to-all-done = bf16[2,32,128]{2,0,1:T(2,128)(2,1)S(1)} async-done(((bf16[2,32,128]{2,0,1:T(2,128)(2,1)}), bf16[2,32,128]{2,0,1:T(2,128)(2,1)S(1)}, u32[]{:S(2)}, u32[]{:S(2)}) %all-to-all-start) | async-done | bytes 16416 | tf_op jit(solution)/shard_map/all_to_all | solution.py:18
  22.8 3.3 %all-to-all-start.1 = ((bf16[2,32,128]{2,0,1:T(2,128)(2,1)}), bf16[2,32,128]{2,0,1:T(2,128)(2,1)S(1)}, u32[]{:S(2)}, u32[]{:S(2)}) async-start(bf16[2,32,128]{2,0,1:T(2,128)(2,1)} %copy.29), calls=%async_computation.1 | async-start | bytes 32768 | tf_op jit(solution)/shard_map/all_to_all | solution.py:19
  27.6 4.1 %all-to-all-done.1 = bf16[2,32,128]{2,0,1:T(2,128)(2,1)S(1)} async-done(((bf16[2,32,128]{2,0,1:T(2,128)(2,1)}), bf16[2,32,128]{2,0,1:T(2,128)(2,1)S(1)}, u32[]{:S(2)}, u32[]{:S(2)}) %all-to-all-start.1) | async-done | bytes 16416 | tf_op jit(solution)/shard_map/all_to_all | solution.py:19
  31.7 3.2 %all-to-all-start.3 = ((f32[2,4,8]{2,0,1:T(2,128)}), f32[2,4,8]{2,0,1:T(2,128)S(1)}, u32[]{:S(2)}, u32[]{:S(2)}) async-start(f32[2,4,8]{2,0,1:T(2,128)} %copy.32), calls=%async_computation.3 | async-start | bytes 8192 | tf_op jit(solution)/shard_map/all_to_all | solution.py:23
  35.0 5.5 %all-to-all-done.3 = f32[2,4,8]{2,0,1:T(2,128)S(1)} async-done(((f32[2,4,8]{2,0,1:T(2,128)}), f32[2,4,8]{2,0,1:T(2,128)S(1)}, u32[]{:S(2)}, u32[]{:S(2)}) %all-to-all-start.3) | async-done | bytes 288 | tf_op jit(solution)/shard_map/all_to_all | solution.py:23
  41.1 60.2 %while.28 = (s32[]{:T(128)}, bf16[8,8,128]{2,0,1:T(8,128)(2,1)S(1)}, bf16[8,8,128]{2,0,1:T(8,128)(2,1)S(1)}, f32[8,8]{1,0:T(8,128)S(1)}, f32[8,8]{1,0:T(8,128)S(...) while((s32[]{:T(128)}, ...), condition=%wide.region_2.3_spmd.clone, body=%wide.region_1.2_spmd.clone.sunk | while | flops 85042200 | bytes 5599483 | solution.py:88
  46.7 3.4 %collective-permute-done.4 = f32[8,8,128]{2,1,0:T(8,128)S(1)} collective-permute-done((f32[8,8,128]{2,1,0:T(8,128)S(1)}, f32[8,8,128]{2,1,0:T(8,128)S(1)}, u32[]{:S(2)}, u32[]{:S(2)}) %collective-permute-start.4) | collective-permute-done | bytes 32800 | tf_op jit(solution)/shard_map/while/body/eval_jaxpr/ppermute | solution.py:9
  54.9 3.3 %collective-permute-done.4 = f32[8,8,128]{2,1,0:T(8,128)S(1)} collective-permute-done((f32[8,8,128]{2,1,0:T(8,128)S(1)}, f32[8,8,128]{2,1,0:T(8,128)S(1)}, u32[]{:S(2)}, u32[]{:S(2)}) %collective-permute-start.4) | collective-permute-done | bytes 32800 | tf_op jit(solution)/shard_map/while/body/eval_jaxpr/ppermute | solution.py:9
  58.3 3.1 %collective-permute-start.3 = (f32[8,8]{1,0:T(8,128)S(1)}, f32[8,8]{1,0:T(8,128)S(1)}, u32[]{:S(2)}, u32[]{:S(2)}) collective-permute-start(f32[8,8]{1,0:T(8,128)S(1)} %copy.80), channel_id=1, source_target_pairs={{0,4},{4,8},{8,12},{12,16},{16,20},{20,24},{24,28},{28,0},{1,5},{5... | collective-permute-start | bytes 776 | tf_op jit(solution)/shard_map/while/body/eval_jaxpr/ppermute | solution.py:9
  63.7 3.5 %collective-permute-done.4 = f32[8,8,128]{2,1,0:T(8,128)S(1)} collective-permute-done((f32[8,8,128]{2,1,0:T(8,128)S(1)}, f32[8,8,128]{2,1,0:T(8,128)S(1)}, u32[]{:S(2)}, u32[]{:S(2)}) %collective-permute-start.4) | collective-permute-done | bytes 32800 | tf_op jit(solution)/shard_map/while/body/eval_jaxpr/ppermute | solution.py:9
  67.4 2.0 %collective-permute-start.3 = (f32[8,8]{1,0:T(8,128)S(1)}, f32[8,8]{1,0:T(8,128)S(1)}, u32[]{:S(2)}, u32[]{:S(2)}) collective-permute-start(f32[8,8]{1,0:T(8,128)S(1)} %copy.80), channel_id=1, source_target_pairs={{0,4},{4,8},{8,12},{12,16},{16,20},{20,24},{24,28},{28,0},{1,5},{5... | collective-permute-start | bytes 776 | tf_op jit(solution)/shard_map/while/body/eval_jaxpr/ppermute | solution.py:9
  71.8 3.5 %collective-permute-done.4 = f32[8,8,128]{2,1,0:T(8,128)S(1)} collective-permute-done((f32[8,8,128]{2,1,0:T(8,128)S(1)}, f32[8,8,128]{2,1,0:T(8,128)S(1)}, u32[]{:S(2)}, u32[]{:S(2)}) %collective-permute-start.4) | collective-permute-done | bytes 32800 | tf_op jit(solution)/shard_map/while/body/eval_jaxpr/ppermute | solution.py:9
  75.4 3.1 %collective-permute-start.3 = (f32[8,8]{1,0:T(8,128)S(1)}, f32[8,8]{1,0:T(8,128)S(1)}, u32[]{:S(2)}, u32[]{:S(2)}) collective-permute-start(f32[8,8]{1,0:T(8,128)S(1)} %copy.80), channel_id=1, source_target_pairs={{0,4},{4,8},{8,12},{12,16},{16,20},{20,24},{24,28},{28,0},{1,5},{5... | collective-permute-start | bytes 776 | tf_op jit(solution)/shard_map/while/body/eval_jaxpr/ppermute | solution.py:9
  80.8 3.5 %collective-permute-done.4 = f32[8,8,128]{2,1,0:T(8,128)S(1)} collective-permute-done((f32[8,8,128]{2,1,0:T(8,128)S(1)}, f32[8,8,128]{2,1,0:T(8,128)S(1)}, u32[]{:S(2)}, u32[]{:S(2)}) %collective-permute-start.4) | collective-permute-done | bytes 32800 | tf_op jit(solution)/shard_map/while/body/eval_jaxpr/ppermute | solution.py:9
  84.4 2.0 %collective-permute-start.3 = (f32[8,8]{1,0:T(8,128)S(1)}, f32[8,8]{1,0:T(8,128)S(1)}, u32[]{:S(2)}, u32[]{:S(2)}) collective-permute-start(f32[8,8]{1,0:T(8,128)S(1)} %copy.80), channel_id=1, source_target_pairs={{0,4},{4,8},{8,12},{12,16},{16,20},{20,24},{24,28},{28,0},{1,5},{5... | collective-permute-start | bytes 776 | tf_op jit(solution)/shard_map/while/body/eval_jaxpr/ppermute | solution.py:9
  88.8 3.5 %collective-permute-done.4 = f32[8,8,128]{2,1,0:T(8,128)S(1)} collective-permute-done((f32[8,8,128]{2,1,0:T(8,128)S(1)}, f32[8,8,128]{2,1,0:T(8,128)S(1)}, u32[]{:S(2)}, u32[]{:S(2)}) %collective-permute-start.4) | collective-permute-done | bytes 32800 | tf_op jit(solution)/shard_map/while/body/eval_jaxpr/ppermute | solution.py:9
  92.4 3.1 %collective-permute-start.3 = (f32[8,8]{1,0:T(8,128)S(1)}, f32[8,8]{1,0:T(8,128)S(1)}, u32[]{:S(2)}, u32[]{:S(2)}) collective-permute-start(f32[8,8]{1,0:T(8,128)S(1)} %copy.80), channel_id=1, source_target_pairs={{0,4},{4,8},{8,12},{12,16},{16,20},{20,24},{24,28},{28,0},{1,5},{5... | collective-permute-start | bytes 776 | tf_op jit(solution)/shard_map/while/body/eval_jaxpr/ppermute | solution.py:9
  97.8 3.5 %collective-permute-done.4 = f32[8,8,128]{2,1,0:T(8,128)S(1)} collective-permute-done((f32[8,8,128]{2,1,0:T(8,128)S(1)}, f32[8,8,128]{2,1,0:T(8,128)S(1)}, u32[]{:S(2)}, u32[]{:S(2)}) %collective-permute-start.4) | collective-permute-done | bytes 32800 | tf_op jit(solution)/shard_map/while/body/eval_jaxpr/ppermute | solution.py:9
  103.7 3.2 %collective-permute-done.5 = bf16[8,8,128]{2,1,0:T(8,128)(2,1)} collective-permute-done((bf16[8,8,128]{2,1,0:T(8,128)(2,1)S(1)}, bf16[8,8,128]{2,1,0:T(8,128)(2,1)}, u32[]{:S(2)}, u32[]{:S(2)}) %collective-permute-start.5) | collective-permute-done | bytes 16416 | tf_op jit(solution)/shard_map/ppermute | solution.py:9
  106.9 3.2 %all-to-all-start.4 = ((bf16[8,8,128]{2,1,0:T(8,128)(2,1)}), bf16[8,8,128]{2,1,0:T(8,128)(2,1)S(1)}, u32[]{:S(2)}, u32[]{:S(2)}) async-start(bf16[8,8,128]{2,1,0:T(8,128)(2,1)} %collective-permute-done.5), calls=%async_computation.4 | async-start | bytes 32768 | tf_op jit(solution)/shard_map/all_to_all | solution.py:99
  111.1 4.6 %all-to-all-done.4 = bf16[8,8,128]{2,1,0:T(8,128)(2,1)S(1)} async-done(((bf16[8,8,128]{2,1,0:T(8,128)(2,1)}), bf16[8,8,128]{2,1,0:T(8,128)(2,1)S(1)}, u32[]{:S(2)}, u32[]{:S(2)}) %all-to-all-start.4) | async-done | bytes 16416 | tf_op jit(solution)/shard_map/all_to_all | solution.py:99
  (194 shorter events, 32.5 us)
Async XLA Ops:
  2.1 11.9 %all-to-all-start.2 = ((f32[2,4,8]{2,0,1:T(2,128)}), f32[2,4,8]{2,0,1:T(2,128)S(1)}, u32[]{:S(2)}, u32[]{:S(2)}) async-start(f32[2,4,8]{2,0,1:T(2,128)} %copy.31), calls=%async_computation.2 | async-start | bytes 8192 | tf_op jit(solution)/shard_map/all_to_all | solution.py:22
  14.0 8.8 %all-to-all-start = ((bf16[2,32,128]{2,0,1:T(2,128)(2,1)}), bf16[2,32,128]{2,0,1:T(2,128)(2,1)S(1)}, u32[]{:S(2)}, u32[]{:S(2)}) async-start(bf16[2,32,128]{2,0,1:T(2,128)(2,1)} %copy.27), calls=%async_computation | async-start | bytes 32768 | tf_op jit(solution)/shard_map/all_to_all | solution.py:18
  22.8 8.8 %all-to-all-start.1 = ((bf16[2,32,128]{2,0,1:T(2,128)(2,1)}), bf16[2,32,128]{2,0,1:T(2,128)(2,1)S(1)}, u32[]{:S(2)}, u32[]{:S(2)}) async-start(bf16[2,32,128]{2,0,1:T(2,128)(2,1)} %copy.29), calls=%async_computation.1 | async-start | bytes 32768 | tf_op jit(solution)/shard_map/all_to_all | solution.py:19
  31.7 8.8 %all-to-all-start.3 = ((f32[2,4,8]{2,0,1:T(2,128)}), f32[2,4,8]{2,0,1:T(2,128)S(1)}, u32[]{:S(2)}, u32[]{:S(2)}) async-start(f32[2,4,8]{2,0,1:T(2,128)} %copy.32), calls=%async_computation.3 | async-start | bytes 8192 | tf_op jit(solution)/shard_map/all_to_all | solution.py:23
  41.1 5.6 %collective-permute-start = (bf16[8,8,128]{2,0,1:T(8,128)(2,1)S(1)}, bf16[8,8,128]{2,0,1:T(8,128)(2,1)S(1)}, u32[]{:S(2)}, u32[]{:S(2)}) collective-permute-start(bf16[8,8,128]{2,0,1:T(8,128)(2,1)S(1)} %copy.77), channel_id=1, source_target_pairs={{0,4},{4,8},{8,12},{12,16},{16,20},{20,24},{24,28},{28,0},{1,5},{5... | collective-permute-start | bytes 49160 | tf_op jit(solution)/shard_map/while/body/eval_jaxpr/ppermute | solution.py:9
  41.1 5.6 %collective-permute-start.1 = (bf16[8,8,128]{2,0,1:T(8,128)(2,1)S(1)}, bf16[8,8,128]{2,0,1:T(8,128)(2,1)S(1)}, u32[]{:S(2)}, u32[]{:S(2)}) collective-permute-start(bf16[8,8,128]{2,0,1:T(8,128)(2,1)S(1)} %copy.78), channel_id=1, source_target_pairs={{0,4},{4,8},{8,12},{12,16},{16,20},{20,24},{24,28},{28,0},{1,5},{5... | collective-permute-start | bytes 49160 | tf_op jit(solution)/shard_map/while/body/eval_jaxpr/ppermute | solution.py:9
  50.2 4.7 %collective-permute-start = (bf16[8,8,128]{2,0,1:T(8,128)(2,1)S(1)}, bf16[8,8,128]{2,0,1:T(8,128)(2,1)S(1)}, u32[]{:S(2)}, u32[]{:S(2)}) collective-permute-start(bf16[8,8,128]{2,0,1:T(8,128)(2,1)S(1)} %copy.77), channel_id=1, source_target_pairs={{0,4},{4,8},{8,12},{12,16},{16,20},{20,24},{24,28},{28,0},{1,5},{5... | collective-permute-start | bytes 49160 | tf_op jit(solution)/shard_map/while/body/eval_jaxpr/ppermute | solution.py:9
  50.2 4.7 %collective-permute-start.1 = (bf16[8,8,128]{2,0,1:T(8,128)(2,1)S(1)}, bf16[8,8,128]{2,0,1:T(8,128)(2,1)S(1)}, u32[]{:S(2)}, u32[]{:S(2)}) collective-permute-start(bf16[8,8,128]{2,0,1:T(8,128)(2,1)S(1)} %copy.78), channel_id=1, source_target_pairs={{0,4},{4,8},{8,12},{12,16},{16,20},{20,24},{24,28},{28,0},{1,5},{5... | collective-permute-start | bytes 49160 | tf_op jit(solution)/shard_map/while/body/eval_jaxpr/ppermute | solution.py:9
  58.2 5.6 %collective-permute-start = (bf16[8,8,128]{2,0,1:T(8,128)(2,1)S(1)}, bf16[8,8,128]{2,0,1:T(8,128)(2,1)S(1)}, u32[]{:S(2)}, u32[]{:S(2)}) collective-permute-start(bf16[8,8,128]{2,0,1:T(8,128)(2,1)S(1)} %copy.77), channel_id=1, source_target_pairs={{0,4},{4,8},{8,12},{12,16},{16,20},{20,24},{24,28},{28,0},{1,5},{5... | collective-permute-start | bytes 49160 | tf_op jit(solution)/shard_map/while/body/eval_jaxpr/ppermute | solution.py:9
  58.2 5.6 %collective-permute-start.1 = (bf16[8,8,128]{2,0,1:T(8,128)(2,1)S(1)}, bf16[8,8,128]{2,0,1:T(8,128)(2,1)S(1)}, u32[]{:S(2)}, u32[]{:S(2)}) collective-permute-start(bf16[8,8,128]{2,0,1:T(8,128)(2,1)S(1)} %copy.78), channel_id=1, source_target_pairs={{0,4},{4,8},{8,12},{12,16},{16,20},{20,24},{24,28},{28,0},{1,5},{5... | collective-permute-start | bytes 49160 | tf_op jit(solution)/shard_map/while/body/eval_jaxpr/ppermute | solution.py:9
  58.3 5.4 %collective-permute-start.2 = (f32[8,8]{1,0:T(8,128)S(1)}, f32[8,8]{1,0:T(8,128)S(1)}, u32[]{:S(2)}, u32[]{:S(2)}) collective-permute-start(f32[8,8]{1,0:T(8,128)S(1)} %copy.79), channel_id=1, source_target_pairs={{0,4},{4,8},{8,12},{12,16},{16,20},{20,24},{24,28},{28,0},{1,5},{5... | collective-permute-start | bytes 776 | tf_op jit(solution)/shard_map/while/body/eval_jaxpr/ppermute | solution.py:9
  58.3 5.4 %collective-permute-start.3 = (f32[8,8]{1,0:T(8,128)S(1)}, f32[8,8]{1,0:T(8,128)S(1)}, u32[]{:S(2)}, u32[]{:S(2)}) collective-permute-start(f32[8,8]{1,0:T(8,128)S(1)} %copy.80), channel_id=1, source_target_pairs={{0,4},{4,8},{8,12},{12,16},{16,20},{20,24},{24,28},{28,0},{1,5},{5... | collective-permute-start | bytes 776 | tf_op jit(solution)/shard_map/while/body/eval_jaxpr/ppermute | solution.py:9
  67.2 4.5 %collective-permute-start = (bf16[8,8,128]{2,0,1:T(8,128)(2,1)S(1)}, bf16[8,8,128]{2,0,1:T(8,128)(2,1)S(1)}, u32[]{:S(2)}, u32[]{:S(2)}) collective-permute-start(bf16[8,8,128]{2,0,1:T(8,128)(2,1)S(1)} %copy.77), channel_id=1, source_target_pairs={{0,4},{4,8},{8,12},{12,16},{16,20},{20,24},{24,28},{28,0},{1,5},{5... | collective-permute-start | bytes 49160 | tf_op jit(solution)/shard_map/while/body/eval_jaxpr/ppermute | solution.py:9
  67.2 4.5 %collective-permute-start.1 = (bf16[8,8,128]{2,0,1:T(8,128)(2,1)S(1)}, bf16[8,8,128]{2,0,1:T(8,128)(2,1)S(1)}, u32[]{:S(2)}, u32[]{:S(2)}) collective-permute-start(bf16[8,8,128]{2,0,1:T(8,128)(2,1)S(1)} %copy.78), channel_id=1, source_target_pairs={{0,4},{4,8},{8,12},{12,16},{16,20},{20,24},{24,28},{28,0},{1,5},{5... | collective-permute-start | bytes 49160 | tf_op jit(solution)/shard_map/while/body/eval_jaxpr/ppermute | solution.py:9
  75.2 5.6 %collective-permute-start = (bf16[8,8,128]{2,0,1:T(8,128)(2,1)S(1)}, bf16[8,8,128]{2,0,1:T(8,128)(2,1)S(1)}, u32[]{:S(2)}, u32[]{:S(2)}) collective-permute-start(bf16[8,8,128]{2,0,1:T(8,128)(2,1)S(1)} %copy.77), channel_id=1, source_target_pairs={{0,4},{4,8},{8,12},{12,16},{16,20},{20,24},{24,28},{28,0},{1,5},{5... | collective-permute-start | bytes 49160 | tf_op jit(solution)/shard_map/while/body/eval_jaxpr/ppermute | solution.py:9
  75.2 5.6 %collective-permute-start.1 = (bf16[8,8,128]{2,0,1:T(8,128)(2,1)S(1)}, bf16[8,8,128]{2,0,1:T(8,128)(2,1)S(1)}, u32[]{:S(2)}, u32[]{:S(2)}) collective-permute-start(bf16[8,8,128]{2,0,1:T(8,128)(2,1)S(1)} %copy.78), channel_id=1, source_target_pairs={{0,4},{4,8},{8,12},{12,16},{16,20},{20,24},{24,28},{28,0},{1,5},{5... | collective-permute-start | bytes 49160 | tf_op jit(solution)/shard_map/while/body/eval_jaxpr/ppermute | solution.py:9
  75.3 5.4 %collective-permute-start.2 = (f32[8,8]{1,0:T(8,128)S(1)}, f32[8,8]{1,0:T(8,128)S(1)}, u32[]{:S(2)}, u32[]{:S(2)}) collective-permute-start(f32[8,8]{1,0:T(8,128)S(1)} %copy.79), channel_id=1, source_target_pairs={{0,4},{4,8},{8,12},{12,16},{16,20},{20,24},{24,28},{28,0},{1,5},{5... | collective-permute-start | bytes 776 | tf_op jit(solution)/shard_map/while/body/eval_jaxpr/ppermute | solution.py:9
  75.4 5.4 %collective-permute-start.3 = (f32[8,8]{1,0:T(8,128)S(1)}, f32[8,8]{1,0:T(8,128)S(1)}, u32[]{:S(2)}, u32[]{:S(2)}) collective-permute-start(f32[8,8]{1,0:T(8,128)S(1)} %copy.80), channel_id=1, source_target_pairs={{0,4},{4,8},{8,12},{12,16},{16,20},{20,24},{24,28},{28,0},{1,5},{5... | collective-permute-start | bytes 776 | tf_op jit(solution)/shard_map/while/body/eval_jaxpr/ppermute | solution.py:9
  84.2 4.5 %collective-permute-start.1 = (bf16[8,8,128]{2,0,1:T(8,128)(2,1)S(1)}, bf16[8,8,128]{2,0,1:T(8,128)(2,1)S(1)}, u32[]{:S(2)}, u32[]{:S(2)}) collective-permute-start(bf16[8,8,128]{2,0,1:T(8,128)(2,1)S(1)} %copy.78), channel_id=1, source_target_pairs={{0,4},{4,8},{8,12},{12,16},{16,20},{20,24},{24,28},{28,0},{1,5},{5... | collective-permute-start | bytes 49160 | tf_op jit(solution)/shard_map/while/body/eval_jaxpr/ppermute | solution.py:9
  92.3 5.6 %collective-permute-start = (bf16[8,8,128]{2,0,1:T(8,128)(2,1)S(1)}, bf16[8,8,128]{2,0,1:T(8,128)(2,1)S(1)}, u32[]{:S(2)}, u32[]{:S(2)}) collective-permute-start(bf16[8,8,128]{2,0,1:T(8,128)(2,1)S(1)} %copy.77), channel_id=1, source_target_pairs={{0,4},{4,8},{8,12},{12,16},{16,20},{20,24},{24,28},{28,0},{1,5},{5... | collective-permute-start | bytes 49160 | tf_op jit(solution)/shard_map/while/body/eval_jaxpr/ppermute | solution.py:9
  92.3 5.6 %collective-permute-start.1 = (bf16[8,8,128]{2,0,1:T(8,128)(2,1)S(1)}, bf16[8,8,128]{2,0,1:T(8,128)(2,1)S(1)}, u32[]{:S(2)}, u32[]{:S(2)}) collective-permute-start(bf16[8,8,128]{2,0,1:T(8,128)(2,1)S(1)} %copy.78), channel_id=1, source_target_pairs={{0,4},{4,8},{8,12},{12,16},{16,20},{20,24},{24,28},{28,0},{1,5},{5... | collective-permute-start | bytes 49160 | tf_op jit(solution)/shard_map/while/body/eval_jaxpr/ppermute | solution.py:9
  92.3 5.5 %collective-permute-start.2 = (f32[8,8]{1,0:T(8,128)S(1)}, f32[8,8]{1,0:T(8,128)S(1)}, u32[]{:S(2)}, u32[]{:S(2)}) collective-permute-start(f32[8,8]{1,0:T(8,128)S(1)} %copy.79), channel_id=1, source_target_pairs={{0,4},{4,8},{8,12},{12,16},{16,20},{20,24},{24,28},{28,0},{1,5},{5... | collective-permute-start | bytes 776 | tf_op jit(solution)/shard_map/while/body/eval_jaxpr/ppermute | solution.py:9
  92.4 5.4 %collective-permute-start.3 = (f32[8,8]{1,0:T(8,128)S(1)}, f32[8,8]{1,0:T(8,128)S(1)}, u32[]{:S(2)}, u32[]{:S(2)}) collective-permute-start(f32[8,8]{1,0:T(8,128)S(1)} %copy.80), channel_id=1, source_target_pairs={{0,4},{4,8},{8,12},{12,16},{16,20},{20,24},{24,28},{28,0},{1,5},{5... | collective-permute-start | bytes 776 | tf_op jit(solution)/shard_map/while/body/eval_jaxpr/ppermute | solution.py:9
  106.9 8.8 %all-to-all-start.4 = ((bf16[8,8,128]{2,1,0:T(8,128)(2,1)}), bf16[8,8,128]{2,1,0:T(8,128)(2,1)S(1)}, u32[]{:S(2)}, u32[]{:S(2)}) async-start(bf16[8,8,128]{2,1,0:T(8,128)(2,1)} %collective-permute-done.5), calls=%async_computation.4 | async-start | bytes 32768 | tf_op jit(solution)/shard_map/all_to_all | solution.py:99
  (28 other events, 128.0 us)
where the time goes:
time: 117 us; the launch traced here: 116 us
  waiting for transfers between devices  50 us (43%)
  starting transfers between devices  39.4 us (34%)
  local copies, waits for them, and re-layouts  12.4 us (11%)
  matrix products  11.5 us (10%)
  other arithmetic  1.51 us (1%)
    ppermute x36, waiting for transfers between devices, shifted(): lax.ppermute(value, axis, [(i, (i + by) % peers) for i in range(peers)])  27.5 us
    ppermute x36, starting transfers between devices, shifted(): lax.ppermute(value, axis, [(i, (i + by) % peers) for i in range(peers)])  20.1 us
    all_to_all x1, starting transfers between devices, local(): lax.all_to_all(log_norms, 'kvh', split_axis=1, concat_axis=0, tiled=True)  6.35 us
    all_to_all x1, waiting for transfers between devices, local(): lax.all_to_all(deltas, 'kvh', split_axis=1, concat_axis=0, tiled=True)  5.48 us
    while x42, local copies, waits for them, and re-layouts  5.07 us
    all_to_all x1, waiting for transfers between devices, local(): lax.all_to_all(query_grad.astype(jnp.bfloat16), 'kvh', split_axis=0, conc...  4.59 us
    all_to_all x1, waiting for transfers between devices, local(): lax.all_to_all(log_norms, 'kvh', split_axis=1, concat_axis=0, tiled=True)  4.21 us
    all_to_all x1, waiting for transfers between devices, local(): lax.all_to_all(queries, 'kvh', split_axis=1, concat_axis=0, tiled=True)  4.16 us
  transfers between devices with their start and end apart: 41, of which 16 were waited for; matrix products, arithmetic and copies ran while one was open for 14% of the time, Pallas kernels for 0%

commit v1 on v0

--- a/solution.py
+++ b/solution.py
@@ -2,6 +2,12 @@
 import jax.numpy as jnp
 from jax import lax
 from jax.sharding import PartitionSpec as P
+
+
+def stacked_exchange(x, name, split, join):
+    pieces = jnp.split(x, lax.axis_size(name), axis=split)
+    got = lax.all_to_all(jnp.stack(pieces), name, 0, 0)
+    return jnp.concatenate(got, axis=join)
 
 
 def shifted(value, axis, by):
@@ -15,7 +21,7 @@
     seq_index = lax.axis_index("seq")
     deltas = jnp.sum(grad_out.astype(jnp.float32) * attn_out.astype(jnp.float32), axis=-1)
     query_block, grad_block = (
-        lax.all_to_all(queries, "kvh", split_axis=1, concat_axis=0, tiled=True),
+        stacked_exchange(queries, "kvh", 1, 0),
         lax.all_to_all(grad_out, "kvh", split_axis=1, concat_axis=0, tiled=True),
     )
     norm_block, delta_block = (

time: 117 us -> 117 us (level)
  local copies, waits for them, and re-layouts: 12.4 us -> 11.1 us
    unnamed x10 -> x9, local copies, waits for them, and re-layouts: 3.33 us -> 2.72 us
  transfers between devices with their start and end apart: 41 -> 41, of which waited for: 16 -> 16; matrix products, arithmetic and copies ran while one was open for 14% -> 13% of each run, Pallas kernels for 0% -> 0%
where the time goes in v1:
time: 117 us; the launch traced here: 116 us
  waiting for transfers between devices  50 us (43%)
  starting transfers between devices  39.5 us (34%)
  matrix products  11.5 us (10%)
  local copies, waits for them, and re-layouts  11.1 us (9%)
  other arithmetic  2.13 us (2%)
    ppermute x36, waiting for transfers between devices, shifted(): lax.ppermute(value, axis, [(i, (i + by) % peers) for i in range(peers)])  27.5 us
    ppermute x36, starting transfers between devices, shifted(): lax.ppermute(value, axis, [(i, (i + by) % peers) for i in range(peers)])  20.2 us
    all_to_all x1, starting transfers between devices, local(): lax.all_to_all(log_norms, 'kvh', split_axis=1, concat_axis=0, tiled=True)  6.35 us
    all_to_all x1, waiting for transfers between devices, local(): lax.all_to_all(deltas, 'kvh', split_axis=1, concat_axis=0, tiled=True)  5.41 us
    while x42, local copies, waits for them, and re-layouts  5.08 us
    all_to_all x1, waiting for transfers between devices, local(): lax.all_to_all(query_grad.astype(jnp.bfloat16), 'kvh', split_axis=0, conc...  4.59 us
    all_to_all x1, waiting for transfers between devices, stacked_exchange(): got = lax.all_to_all(jnp.stack(pieces), name, 0, 0)  4.23 us
    all_to_all x1, waiting for transfers between devices, local(): lax.all_to_all(grad_out, 'kvh', split_axis=1, concat_axis=0, tiled=True)  4.15 us
  transfers between devices with their start and end apart: 41, of which 16 were waited for; matrix products, arithmetic and copies ran while one was open for 13% of the time, Pallas kernels for 0%

profile of v1, /device:TPU:0, one launch (start us, length us, event | category | flops | bytes accessed | tf_op | source)
XLA Modules:
  0.0 115.7 jit_solution(5973198369871653567)
XLA Ops:
  2.1 6.3 %all-to-all-start.2 = ((f32[2,4,8]{2,0,1:T(2,128)}), f32[2,4,8]{2,0,1:T(2,128)S(1)}, u32[]{:S(2)}, u32[]{:S(2)}) async-start(f32[2,4,8]{2,0,1:T(2,128)} %copy.30), calls=%async_computation.2 | async-start | bytes 8192 | tf_op jit(solution)/shard_map/all_to_all | solution.py:28
  9.8 4.1 %all-to-all-done.2 = f32[2,4,8]{2,0,1:T(2,128)S(1)} async-done(((f32[2,4,8]{2,0,1:T(2,128)}), f32[2,4,8]{2,0,1:T(2,128)S(1)}, u32[]{:S(2)}, u32[]{:S(2)}) %all-to-all-start.2) | async-done | bytes 288 | tf_op jit(solution)/shard_map/all_to_all | solution.py:28
  14.0 3.3 %all-to-all-start = ((bf16[4,2,8,128]{3,2,1,0:T(8,128)(2,1)}), bf16[4,2,8,128]{3,2,1,0:T(8,128)(2,1)S(1)}, u32[]{:S(2)}, u32[]{:S(2)}) async-start(bf16[4,2,8,128]{3,2,1,0:T(8,128)(2,1)} %pad_maximum_fusion), calls=%async_computation | async-start | bytes 32768 | tf_op jit(solution)/shard_map/all_to_all | solution.py:9
  18.6 4.2 %all-to-all-done = bf16[4,2,8,128]{3,2,1,0:T(8,128)(2,1)S(1)} async-done(((bf16[4,2,8,128]{3,2,1,0:T(8,128)(2,1)}), bf16[4,2,8,128]{3,2,1,0:T(8,128)(2,1)S(1)}, u32[]{:S(2)}, u32[]{:S(2)}) %all-to-all-start) | async-done | bytes 16416 | tf_op jit(solution)/shard_map/all_to_all | solution.py:9
  22.8 3.3 %all-to-all-start.1 = ((bf16[2,32,128]{2,0,1:T(2,128)(2,1)}), bf16[2,32,128]{2,0,1:T(2,128)(2,1)S(1)}, u32[]{:S(2)}, u32[]{:S(2)}) async-start(bf16[2,32,128]{2,0,1:T(2,128)(2,1)} %copy.28), calls=%async_computation.1 | async-start | bytes 32768 | tf_op jit(solution)/shard_map/all_to_all | solution.py:25
  27.5 4.1 %all-to-all-done.1 = bf16[2,32,128]{2,0,1:T(2,128)(2,1)S(1)} async-done(((bf16[2,32,128]{2,0,1:T(2,128)(2,1)}), bf16[2,32,128]{2,0,1:T(2,128)(2,1)S(1)}, u32[]{:S(2)}, u32[]{:S(2)}) %all-to-all-start.1) | async-done | bytes 16416 | tf_op jit(solution)/shard_map/all_to_all | solution.py:25
  31.7 3.2 %all-to-all-start.3 = ((f32[2,4,8]{2,0,1:T(2,128)}), f32[2,4,8]{2,0,1:T(2,128)S(1)}, u32[]{:S(2)}, u32[]{:S(2)}) async-start(f32[2,4,8]{2,0,1:T(2,128)} %copy.31), calls=%async_computation.3 | async-start | bytes 8192 | tf_op jit(solution)/shard_map/all_to_all | solution.py:29
  35.1 5.4 %all-to-all-done.3 = f32[2,4,8]{2,0,1:T(2,128)S(1)} async-done(((f32[2,4,8]{2,0,1:T(2,128)}), f32[2,4,8]{2,0,1:T(2,128)S(1)}, u32[]{:S(2)}, u32[]{:S(2)}) %all-to-all-start.3) | async-done | bytes 288 | tf_op jit(solution)/shard_map/all_to_all | solution.py:29
  40.5 60.2 %while.28 = (s32[]{:T(128)}, bf16[8,8,128]{2,0,1:T(8,128)(2,1)S(1)}, bf16[8,8,128]{2,0,1:T(8,128)(2,1)S(1)}, f32[8,8]{1,0:T(8,128)S(1)}, f32[8,8]{1,0:T(8,128)S(...) while((s32[]{:T(128)}, ...), condition=%wide.region_2.3_spmd.clone, body=%wide.region_1.2_spmd.clone.sunk | while | flops 85042200 | bytes 5599483 | solution.py:94
  46.2 3.4 %collective-permute-done.4 = f32[8,8,128]{2,1,0:T(8,128)S(1)} collective-permute-done((f32[8,8,128]{2,1,0:T(8,128)S(1)}, f32[8,8,128]{2,1,0:T(8,128)S(1)}, u32[]{:S(2)}, u32[]{:S(2)}) %collective-permute-start.4) | collective-permute-done | bytes 32800 | tf_op jit(solution)/shard_map/while/body/eval_jaxpr/ppermute | solution.py:15
  54.3 3.3 %collective-permute-done.4 = f32[8,8,128]{2,1,0:T(8,128)S(1)} collective-permute-done((f32[8,8,128]{2,1,0:T(8,128)S(1)}, f32[8,8,128]{2,1,0:T(8,128)S(1)}, u32[]{:S(2)}, u32[]{:S(2)}) %collective-permute-start.4) | collective-permute-done | bytes 32800 | tf_op jit(solution)/shard_map/while/body/eval_jaxpr/ppermute | solution.py:15
  57.7 3.1 %collective-permute-start.3 = (f32[8,8]{1,0:T(8,128)S(1)}, f32[8,8]{1,0:T(8,128)S(1)}, u32[]{:S(2)}, u32[]{:S(2)}) collective-permute-start(f32[8,8]{1,0:T(8,128)S(1)} %copy.79), channel_id=1, source_target_pairs={{0,4},{4,8},{8,12},{12,16},{16,20},{20,24},{24,28},{28,0},{1,5},{5... | collective-permute-start | bytes 776 | tf_op jit(solution)/shard_map/while/body/eval_jaxpr/ppermute | solution.py:15
  63.1 3.5 %collective-permute-done.4 = f32[8,8,128]{2,1,0:T(8,128)S(1)} collective-permute-done((f32[8,8,128]{2,1,0:T(8,128)S(1)}, f32[8,8,128]{2,1,0:T(8,128)S(1)}, u32[]{:S(2)}, u32[]{:S(2)}) %collective-permute-start.4) | collective-permute-done | bytes 32800 | tf_op jit(solution)/shard_map/while/body/eval_jaxpr/ppermute | solution.py:15
  66.8 2.0 %collective-permute-start.3 = (f32[8,8]{1,0:T(8,128)S(1)}, f32[8,8]{1,0:T(8,128)S(1)}, u32[]{:S(2)}, u32[]{:S(2)}) collective-permute-start(f32[8,8]{1,0:T(8,128)S(1)} %copy.79), channel_id=1, source_target_pairs={{0,4},{4,8},{8,12},{12,16},{16,20},{20,24},{24,28},{28,0},{1,5},{5... | collective-permute-start | bytes 776 | tf_op jit(solution)/shard_map/while/body/eval_jaxpr/ppermute | solution.py:15
  71.2 3.5 %collective-permute-done.4 = f32[8,8,128]{2,1,0:T(8,128)S(1)} collective-permute-done((f32[8,8,128]{2,1,0:T(8,128)S(1)}, f32[8,8,128]{2,1,0:T(8,128)S(1)}, u32[]{:S(2)}, u32[]{:S(2)}) %collective-permute-start.4) | collective-permute-done | bytes 32800 | tf_op jit(solution)/shard_map/while/body/eval_jaxpr/ppermute | solution.py:15
  74.8 3.1 %collective-permute-start.3 = (f32[8,8]{1,0:T(8,128)S(1)}, f32[8,8]{1,0:T(8,128)S(1)}, u32[]{:S(2)}, u32[]{:S(2)}) collective-permute-start(f32[8,8]{1,0:T(8,128)S(1)} %copy.79), channel_id=1, source_target_pairs={{0,4},{4,8},{8,12},{12,16},{16,20},{20,24},{24,28},{28,0},{1,5},{5... | collective-permute-start | bytes 776 | tf_op jit(solution)/shard_map/while/body/eval_jaxpr/ppermute | solution.py:15
  80.2 3.5 %collective-permute-done.4 = f32[8,8,128]{2,1,0:T(8,128)S(1)} collective-permute-done((f32[8,8,128]{2,1,0:T(8,128)S(1)}, f32[8,8,128]{2,1,0:T(8,128)S(1)}, u32[]{:S(2)}, u32[]{:S(2)}) %collective-permute-start.4) | collective-permute-done | bytes 32800 | tf_op jit(solution)/shard_map/while/body/eval_jaxpr/ppermute | solution.py:15
  83.8 2.0 %collective-permute-start.3 = (f32[8,8]{1,0:T(8,128)S(1)}, f32[8,8]{1,0:T(8,128)S(1)}, u32[]{:S(2)}, u32[]{:S(2)}) collective-permute-start(f32[8,8]{1,0:T(8,128)S(1)} %copy.79), channel_id=1, source_target_pairs={{0,4},{4,8},{8,12},{12,16},{16,20},{20,24},{24,28},{28,0},{1,5},{5... | collective-permute-start | bytes 776 | tf_op jit(solution)/shard_map/while/body/eval_jaxpr/ppermute | solution.py:15
  88.2 3.5 %collective-permute-done.4 = f32[8,8,128]{2,1,0:T(8,128)S(1)} collective-permute-done((f32[8,8,128]{2,1,0:T(8,128)S(1)}, f32[8,8,128]{2,1,0:T(8,128)S(1)}, u32[]{:S(2)}, u32[]{:S(2)}) %collective-permute-start.4) | collective-permute-done | bytes 32800 | tf_op jit(solution)/shard_map/while/body/eval_jaxpr/ppermute | solution.py:15
  91.8 3.1 %collective-permute-start.3 = (f32[8,8]{1,0:T(8,128)S(1)}, f32[8,8]{1,0:T(8,128)S(1)}, u32[]{:S(2)}, u32[]{:S(2)}) collective-permute-start(f32[8,8]{1,0:T(8,128)S(1)} %copy.79), channel_id=1, source_target_pairs={{0,4},{4,8},{8,12},{12,16},{16,20},{20,24},{24,28},{28,0},{1,5},{5... | collective-permute-start | bytes 776 | tf_op jit(solution)/shard_map/while/body/eval_jaxpr/ppermute | solution.py:15
  97.2 3.5 %collective-permute-done.4 = f32[8,8,128]{2,1,0:T(8,128)S(1)} collective-permute-done((f32[8,8,128]{2,1,0:T(8,128)S(1)}, f32[8,8,128]{2,1,0:T(8,128)S(1)}, u32[]{:S(2)}, u32[]{:S(2)}) %collective-permute-start.4) | collective-permute-done | bytes 32800 | tf_op jit(solution)/shard_map/while/body/eval_jaxpr/ppermute | solution.py:15
  103.1 3.2 %collective-permute-done.5 = bf16[8,8,128]{2,1,0:T(8,128)(2,1)} collective-permute-done((bf16[8,8,128]{2,1,0:T(8,128)(2,1)S(1)}, bf16[8,8,128]{2,1,0:T(8,128)(2,1)}, u32[]{:S(2)}, u32[]{:S(2)}) %collective-permute-start.5) | collective-permute-done | bytes 16416 | tf_op jit(solution)/shard_map/ppermute | solution.py:15
  106.3 3.2 %all-to-all-start.4 = ((bf16[8,8,128]{2,1,0:T(8,128)(2,1)}), bf16[8,8,128]{2,1,0:T(8,128)(2,1)S(1)}, u32[]{:S(2)}, u32[]{:S(2)}) async-start(bf16[8,8,128]{2,1,0:T(8,128)(2,1)} %collective-permute-done.5), calls=%async_computation.4 | async-start | bytes 32768 | tf_op jit(solution)/shard_map/all_to_all | solution.py:105
  110.5 4.6 %all-to-all-done.4 = bf16[8,8,128]{2,1,0:T(8,128)(2,1)S(1)} async-done(((bf16[8,8,128]{2,1,0:T(8,128)(2,1)}), bf16[8,8,128]{2,1,0:T(8,128)(2,1)S(1)}, u32[]{:S(2)}, u32[]{:S(2)}) %all-to-all-start.4) | async-done | bytes 16416 | tf_op jit(solution)/shard_map/all_to_all | solution.py:105
  (195 shorter events, 31.9 us)
Async XLA Ops:
  2.1 11.9 %all-to-all-start.2 = ((f32[2,4,8]{2,0,1:T(2,128)}), f32[2,4,8]{2,0,1:T(2,128)S(1)}, u32[]{:S(2)}, u32[]{:S(2)}) async-start(f32[2,4,8]{2,0,1:T(2,128)} %copy.30), calls=%async_computation.2 | async-start | bytes 8192 | tf_op jit(solution)/shard_map/all_to_all | solution.py:28
  14.0 8.8 %all-to-all-start = ((bf16[4,2,8,128]{3,2,1,0:T(8,128)(2,1)}), bf16[4,2,8,128]{3,2,1,0:T(8,128)(2,1)S(1)}, u32[]{:S(2)}, u32[]{:S(2)}) async-start(bf16[4,2,8,128]{3,2,1,0:T(8,128)(2,1)} %pad_maximum_fusion), calls=%async_computation | async-start | bytes 32768 | tf_op jit(solution)/shard_map/all_to_all | solution.py:9
  22.8 8.8 %all-to-all-start.1 = ((bf16[2,32,128]{2,0,1:T(2,128)(2,1)}), bf16[2,32,128]{2,0,1:T(2,128)(2,1)S(1)}, u32[]{:S(2)}, u32[]{:S(2)}) async-start(bf16[2,32,128]{2,0,1:T(2,128)(2,1)} %copy.28), calls=%async_computation.1 | async-start | bytes 32768 | tf_op jit(solution)/shard_map/all_to_all | solution.py:25
  31.7 8.8 %all-to-all-start.3 = ((f32[2,4,8]{2,0,1:T(2,128)}), f32[2,4,8]{2,0,1:T(2,128)S(1)}, u32[]{:S(2)}, u32[]{:S(2)}) async-start(f32[2,4,8]{2,0,1:T(2,128)} %copy.31), calls=%async_computation.3 | async-start | bytes 8192 | tf_op jit(solution)/shard_map/all_to_all | solution.py:29
  40.5 5.7 %collective-permute-start = (bf16[8,8,128]{2,0,1:T(8,128)(2,1)S(1)}, bf16[8,8,128]{2,0,1:T(8,128)(2,1)S(1)}, u32[]{:S(2)}, u32[]{:S(2)}) collective-permute-start(bf16[8,8,128]{2,0,1:T(8,128)(2,1)S(1)} %copy.76), channel_id=1, source_target_pairs={{0,4},{4,8},{8,12},{12,16},{16,20},{20,24},{24,28},{28,0},{1,5},{5... | collective-permute-start | bytes 49160 | tf_op jit(solution)/shard_map/while/body/eval_jaxpr/ppermute | solution.py:15
  40.6 5.6 %collective-permute-start.1 = (bf16[8,8,128]{2,0,1:T(8,128)(2,1)S(1)}, bf16[8,8,128]{2,0,1:T(8,128)(2,1)S(1)}, u32[]{:S(2)}, u32[]{:S(2)}) collective-permute-start(bf16[8,8,128]{2,0,1:T(8,128)(2,1)S(1)} %copy.77), channel_id=1, source_target_pairs={{0,4},{4,8},{8,12},{12,16},{16,20},{20,24},{24,28},{28,0},{1,5},{5... | collective-permute-start | bytes 49160 | tf_op jit(solution)/shard_map/while/body/eval_jaxpr/ppermute | solution.py:15
  49.6 4.7 %collective-permute-start = (bf16[8,8,128]{2,0,1:T(8,128)(2,1)S(1)}, bf16[8,8,128]{2,0,1:T(8,128)(2,1)S(1)}, u32[]{:S(2)}, u32[]{:S(2)}) collective-permute-start(bf16[8,8,128]{2,0,1:T(8,128)(2,1)S(1)} %copy.76), channel_id=1, source_target_pairs={{0,4},{4,8},{8,12},{12,16},{16,20},{20,24},{24,28},{28,0},{1,5},{5... | collective-permute-start | bytes 49160 | tf_op jit(solution)/shard_map/while/body/eval_jaxpr/ppermute | solution.py:15
  49.6 4.7 %collective-permute-start.1 = (bf16[8,8,128]{2,0,1:T(8,128)(2,1)S(1)}, bf16[8,8,128]{2,0,1:T(8,128)(2,1)S(1)}, u32[]{:S(2)}, u32[]{:S(2)}) collective-permute-start(bf16[8,8,128]{2,0,1:T(8,128)(2,1)S(1)} %copy.77), channel_id=1, source_target_pairs={{0,4},{4,8},{8,12},{12,16},{16,20},{20,24},{24,28},{28,0},{1,5},{5... | collective-permute-start | bytes 49160 | tf_op jit(solution)/shard_map/while/body/eval_jaxpr/ppermute | solution.py:15
  57.6 5.6 %collective-permute-start = (bf16[8,8,128]{2,0,1:T(8,128)(2,1)S(1)}, bf16[8,8,128]{2,0,1:T(8,128)(2,1)S(1)}, u32[]{:S(2)}, u32[]{:S(2)}) collective-permute-start(bf16[8,8,128]{2,0,1:T(8,128)(2,1)S(1)} %copy.76), channel_id=1, source_target_pairs={{0,4},{4,8},{8,12},{12,16},{16,20},{20,24},{24,28},{28,0},{1,5},{5... | collective-permute-start | bytes 49160 | tf_op jit(solution)/shard_map/while/body/eval_jaxpr/ppermute | solution.py:15
  57.6 5.6 %collective-permute-start.1 = (bf16[8,8,128]{2,0,1:T(8,128)(2,1)S(1)}, bf16[8,8,128]{2,0,1:T(8,128)(2,1)S(1)}, u32[]{:S(2)}, u32[]{:S(2)}) collective-permute-start(bf16[8,8,128]{2,0,1:T(8,128)(2,1)S(1)} %copy.77), channel_id=1, source_target_pairs={{0,4},{4,8},{8,12},{12,16},{16,20},{20,24},{24,28},{28,0},{1,5},{5... | collective-permute-start | bytes 49160 | tf_op jit(solution)/shard_map/while/body/eval_jaxpr/ppermute | solution.py:15
  57.7 5.4 %collective-permute-start.2 = (f32[8,8]{1,0:T(8,128)S(1)}, f32[8,8]{1,0:T(8,128)S(1)}, u32[]{:S(2)}, u32[]{:S(2)}) collective-permute-start(f32[8,8]{1,0:T(8,128)S(1)} %copy.78), channel_id=1, source_target_pairs={{0,4},{4,8},{8,12},{12,16},{16,20},{20,24},{24,28},{28,0},{1,5},{5... | collective-permute-start | bytes 776 | tf_op jit(solution)/shard_map/while/body/eval_jaxpr/ppermute | solution.py:15
  57.7 5.4 %collective-permute-start.3 = (f32[8,8]{1,0:T(8,128)S(1)}, f32[8,8]{1,0:T(8,128)S(1)}, u32[]{:S(2)}, u32[]{:S(2)}) collective-permute-start(f32[8,8]{1,0:T(8,128)S(1)} %copy.79), channel_id=1, source_target_pairs={{0,4},{4,8},{8,12},{12,16},{16,20},{20,24},{24,28},{28,0},{1,5},{5... | collective-permute-start | bytes 776 | tf_op jit(solution)/shard_map/while/body/eval_jaxpr/ppermute | solution.py:15
  66.6 4.5 %collective-permute-start = (bf16[8,8,128]{2,0,1:T(8,128)(2,1)S(1)}, bf16[8,8,128]{2,0,1:T(8,128)(2,1)S(1)}, u32[]{:S(2)}, u32[]{:S(2)}) collective-permute-start(bf16[8,8,128]{2,0,1:T(8,128)(2,1)S(1)} %copy.76), channel_id=1, source_target_pairs={{0,4},{4,8},{8,12},{12,16},{16,20},{20,24},{24,28},{28,0},{1,5},{5... | collective-permute-start | bytes 49160 | tf_op jit(solution)/shard_map/while/body/eval_jaxpr/ppermute | solution.py:15
  66.6 4.5 %collective-permute-start.1 = (bf16[8,8,128]{2,0,1:T(8,128)(2,1)S(1)}, bf16[8,8,128]{2,0,1:T(8,128)(2,1)S(1)}, u32[]{:S(2)}, u32[]{:S(2)}) collective-permute-start(bf16[8,8,128]{2,0,1:T(8,128)(2,1)S(1)} %copy.77), channel_id=1, source_target_pairs={{0,4},{4,8},{8,12},{12,16},{16,20},{20,24},{24,28},{28,0},{1,5},{5... | collective-permute-start | bytes 49160 | tf_op jit(solution)/shard_map/while/body/eval_jaxpr/ppermute | solution.py:15
  74.6 5.6 %collective-permute-start = (bf16[8,8,128]{2,0,1:T(8,128)(2,1)S(1)}, bf16[8,8,128]{2,0,1:T(8,128)(2,1)S(1)}, u32[]{:S(2)}, u32[]{:S(2)}) collective-permute-start(bf16[8,8,128]{2,0,1:T(8,128)(2,1)S(1)} %copy.76), channel_id=1, source_target_pairs={{0,4},{4,8},{8,12},{12,16},{16,20},{20,24},{24,28},{28,0},{1,5},{5... | collective-permute-start | bytes 49160 | tf_op jit(solution)/shard_map/while/body/eval_jaxpr/ppermute | solution.py:15
  74.6 5.6 %collective-permute-start.1 = (bf16[8,8,128]{2,0,1:T(8,128)(2,1)S(1)}, bf16[8,8,128]{2,0,1:T(8,128)(2,1)S(1)}, u32[]{:S(2)}, u32[]{:S(2)}) collective-permute-start(bf16[8,8,128]{2,0,1:T(8,128)(2,1)S(1)} %copy.77), channel_id=1, source_target_pairs={{0,4},{4,8},{8,12},{12,16},{16,20},{20,24},{24,28},{28,0},{1,5},{5... | collective-permute-start | bytes 49160 | tf_op jit(solution)/shard_map/while/body/eval_jaxpr/ppermute | solution.py:15
  74.7 5.4 %collective-permute-start.2 = (f32[8,8]{1,0:T(8,128)S(1)}, f32[8,8]{1,0:T(8,128)S(1)}, u32[]{:S(2)}, u32[]{:S(2)}) collective-permute-start(f32[8,8]{1,0:T(8,128)S(1)} %copy.78), channel_id=1, source_target_pairs={{0,4},{4,8},{8,12},{12,16},{16,20},{20,24},{24,28},{28,0},{1,5},{5... | collective-permute-start | bytes 776 | tf_op jit(solution)/shard_map/while/body/eval_jaxpr/ppermute | solution.py:15
  74.8 5.4 %collective-permute-start.3 = (f32[8,8]{1,0:T(8,128)S(1)}, f32[8,8]{1,0:T(8,128)S(1)}, u32[]{:S(2)}, u32[]{:S(2)}) collective-permute-start(f32[8,8]{1,0:T(8,128)S(1)} %copy.79), channel_id=1, source_target_pairs={{0,4},{4,8},{8,12},{12,16},{16,20},{20,24},{24,28},{28,0},{1,5},{5... | collective-permute-start | bytes 776 | tf_op jit(solution)/shard_map/while/body/eval_jaxpr/ppermute | solution.py:15
  83.7 4.5 %collective-permute-start.1 = (bf16[8,8,128]{2,0,1:T(8,128)(2,1)S(1)}, bf16[8,8,128]{2,0,1:T(8,128)(2,1)S(1)}, u32[]{:S(2)}, u32[]{:S(2)}) collective-permute-start(bf16[8,8,128]{2,0,1:T(8,128)(2,1)S(1)} %copy.77), channel_id=1, source_target_pairs={{0,4},{4,8},{8,12},{12,16},{16,20},{20,24},{24,28},{28,0},{1,5},{5... | collective-permute-start | bytes 49160 | tf_op jit(solution)/shard_map/while/body/eval_jaxpr/ppermute | solution.py:15
  91.7 5.6 %collective-permute-start = (bf16[8,8,128]{2,0,1:T(8,128)(2,1)S(1)}, bf16[8,8,128]{2,0,1:T(8,128)(2,1)S(1)}, u32[]{:S(2)}, u32[]{:S(2)}) collective-permute-start(bf16[8,8,128]{2,0,1:T(8,128)(2,1)S(1)} %copy.76), channel_id=1, source_target_pairs={{0,4},{4,8},{8,12},{12,16},{16,20},{20,24},{24,28},{28,0},{1,5},{5... | collective-permute-start | bytes 49160 | tf_op jit(solution)/shard_map/while/body/eval_jaxpr/ppermute | solution.py:15
  91.7 5.6 %collective-permute-start.1 = (bf16[8,8,128]{2,0,1:T(8,128)(2,1)S(1)}, bf16[8,8,128]{2,0,1:T(8,128)(2,1)S(1)}, u32[]{:S(2)}, u32[]{:S(2)}) collective-permute-start(bf16[8,8,128]{2,0,1:T(8,128)(2,1)S(1)} %copy.77), channel_id=1, source_target_pairs={{0,4},{4,8},{8,12},{12,16},{16,20},{20,24},{24,28},{28,0},{1,5},{5... | collective-permute-start | bytes 49160 | tf_op jit(solution)/shard_map/while/body/eval_jaxpr/ppermute | solution.py:15
  91.7 5.4 %collective-permute-start.2 = (f32[8,8]{1,0:T(8,128)S(1)}, f32[8,8]{1,0:T(8,128)S(1)}, u32[]{:S(2)}, u32[]{:S(2)}) collective-permute-start(f32[8,8]{1,0:T(8,128)S(1)} %copy.78), channel_id=1, source_target_pairs={{0,4},{4,8},{8,12},{12,16},{16,20},{20,24},{24,28},{28,0},{1,5},{5... | collective-permute-start | bytes 776 | tf_op jit(solution)/shard_map/while/body/eval_jaxpr/ppermute | solution.py:15
  91.8 5.4 %collective-permute-start.3 = (f32[8,8]{1,0:T(8,128)S(1)}, f32[8,8]{1,0:T(8,128)S(1)}, u32[]{:S(2)}, u32[]{:S(2)}) collective-permute-start(f32[8,8]{1,0:T(8,128)S(1)} %copy.79), channel_id=1, source_target_pairs={{0,4},{4,8},{8,12},{12,16},{16,20},{20,24},{24,28},{28,0},{1,5},{5... | collective-permute-start | bytes 776 | tf_op jit(solution)/shard_map/while/body/eval_jaxpr/ppermute | solution.py:15
  106.3 8.8 %all-to-all-start.4 = ((bf16[8,8,128]{2,1,0:T(8,128)(2,1)}), bf16[8,8,128]{2,1,0:T(8,128)(2,1)S(1)}, u32[]{:S(2)}, u32[]{:S(2)}) async-start(bf16[8,8,128]{2,1,0:T(8,128)(2,1)} %collective-permute-done.5), calls=%async_computation.4 | async-start | bytes 32768 | tf_op jit(solution)/shard_map/all_to_all | solution.py:105
  (28 other events, 128.0 us)
